TPU v7x, 32 devices: a whole 2x2x4 slice. The times are simulated.
32 devices in a mesh: row: 4 (over y, core), col: 8 (over z, x).
Axes of the slice: x: 2, y: 2, z: 4, core: 2. Of those that a mesh axis runs over, the one named last changes fastest.
Arguments:
- root_inverse: bfloat16 [2048, 2048], P('col', 'row'), may hold values from -1 to 3, as said below
- lower_panels: bfloat16 [4, 1536, 1024], P(None, 'col', 'row'), may hold values from -0.375 to 0.375
- struct_blocks: int32 [4, 12], replicated, may hold values from 0 to 15, as said below
- struct_count: int32 [4], replicated, may hold values from 1 to 12, 32 in all
- diag_inverse: float32 [4, 1024, 1024], P(None, 'col', 'row'), may hold values from -1 to 3, as said below
Outputs:
- offdiag: bfloat16 [4, 1536, 1024], P(None, 'col', 'row')
- diag_block: float32 [4, 1024, 1024], P(None, 'col', 'row')
Inputs may be any that keep to these rules, and one draw needn't show every extreme that they name: `struct_blocks`: each row holds 12 different block numbers of the top supernode; supernode c uses the first struct_count[c] of them. `struct_count`: the counts sum to 32; the largest equals 12. `root_inverse`: Symmetric, with a dominant diagonal. `diag_inverse`: each supernode's block is symmetric; diagonal entries lie between 0.85 and 2.15, all other entries within 0.13 of zero.
All inputs are finite; a program needn't handle non-finite values.
Results may differ from a plain program's by a relative error of at most 0.0095.
Values may be sent and summed in bfloat16 or wider, within the bound.
A program may use at most 64 MiB of HBM per device.

v0:
```python
import jax
import jax.numpy as jnp
from jax import lax
from jax.sharding import PartitionSpec as P

BLOCK = 128
NSMAX = 12


def body(root_inverse, lower_panels, struct_blocks, struct_count, diag_inverse):
    col_index = lax.axis_index("col")
    root_panel = lax.all_gather(root_inverse, "row", axis=1, tiled=True)
    root_width = root_panel.shape[1]
    block_count = root_width // BLOCK
    own_rows = root_panel.shape[0]
    per_dev = own_rows // BLOCK
    local_packed = lower_panels.shape[1]

    def solve_group(lower_group, block_lists, block_counts, inverse_group):
        group_size = lower_group.shape[0]
        cols_here = lower_group.shape[2]
        gathered = lax.all_gather(lower_group, "col", axis=1, tiled=True)
        packed_total = gathered.shape[1]
        full_mask = jnp.arange(packed_total)[None, :] // BLOCK < block_counts[:, None]
        gathered = gathered * full_mask[:, :, None].astype(jnp.bfloat16)
        in_use = jnp.arange(NSMAX)[None, :] < block_counts[:, None]
        onehot = (
            (block_lists[:, None, :] == jnp.arange(block_count)[None, :, None]) & in_use[:, None, :]
        ).astype(jnp.bfloat16)
        spread = jnp.einsum(
            "gbk,gkic->gbic",
            onehot,
            gathered.reshape(group_size, NSMAX, BLOCK, cols_here),
            preferred_element_type=jnp.float32,
        )
        spread = spread.astype(jnp.bfloat16).reshape(group_size, root_width, cols_here)
        root_part = -jnp.einsum(
            "rw,gwc->grc", root_panel, spread, preferred_element_type=jnp.float32
        )
        packed_index = col_index * local_packed + jnp.arange(local_packed)
        local_mask = packed_index[None, :] // BLOCK < block_counts[:, None]
        own_select = lax.dynamic_slice_in_dim(onehot, col_index * per_dev, per_dev, 1).astype(
            jnp.float32
        )
        selected = jnp.einsum(
            "gjk,gjic->gkic",
            own_select,
            root_part.reshape(group_size, per_dev, BLOCK, cols_here),
            precision=lax.Precision.HIGHEST,
            preferred_element_type=jnp.float32,
        )
        selected = selected.reshape(group_size, packed_total, cols_here)
        offdiag = lax.psum_scatter(
            selected.astype(jnp.bfloat16), "col", scatter_dimension=1, tiled=True
        )
        full_cols = lax.all_gather(lower_group, "row", axis=2, tiled=True)
        masked_rows = full_cols * local_mask[:, :, None].astype(jnp.bfloat16)
        schur_terms = jnp.einsum(
            "gka,gkc->gac", masked_rows, offdiag, preferred_element_type=jnp.float32
        )
        schur_part = lax.psum_scatter(
            schur_terms.astype(jnp.bfloat16), "col", scatter_dimension=1, tiled=True
        ).astype(jnp.float32)
        return (offdiag, inverse_group - schur_part)

    group_size = 4
    turn_count = lower_panels.shape[0] // group_size

    def regroup(source_array):
        return source_array.reshape((turn_count, group_size) + source_array.shape[1:])

    def one_turn(running, inputs_now):
        return (running, solve_group(*inputs_now))

    finished, outputs = lax.scan(
        one_turn,
        jnp.int32(0),
        (
            regroup(lower_panels),
            regroup(struct_blocks),
            regroup(struct_count),
            regroup(diag_inverse),
        ),
    )
    offdiag_all, diag_all = outputs
    return (offdiag_all.reshape(lower_panels.shape), diag_all.reshape(diag_inverse.shape))


def solution(mesh):
    in_specs = (P("col", "row"), P(None, "col", "row"), P(), P(), P(None, "col", "row"))
    out_specs = (P(None, "col", "row"), P(None, "col", "row"))
    return jax.shard_map(body, mesh=mesh, in_specs=in_specs, out_specs=out_specs, check_vma=False)
```

profile of v0, /device:TPU:0, one launch (start us, length us, event | category | flops | bytes accessed | tf_op | source)
XLA Modules:
  0.0 269.8 jit_solution(14597254614823216027)
XLA Ops:
  7.2 0.7 all-gather.4.cloned.1.call-update
  7.9 0.0 all-gather.6.cloned.1.call-start
  7.9 0.7 all-gather.6.cloned.1.call-update
  8.7 0.7 all-gather.8.cloned.1.call-update
  9.4 0.0 reduce-scatter.3.cloned.1.call-start
  9.4 0.7 iota_compare_fusion.1
  10.2 0.7 fusion.9
  10.9 0.7 compare_convert_fusion
  11.6 61.3 %all-gather.4.cloned.1.call-done = bf16[4,1536,256]{2,1,0:T(8,128)(2,1)} async-done(((bf16[4,192,256]{2,1,0:T(8,128)(2,1)}), bf16[4,1536,256]{2,1,0:T(8,128)(2,1)}) %all-gather.4.cloned.1.call-update) | async-done | bytes 3145744 | tf_op jit(solution)/shard_map/while/body/eval_jaxpr/all_gather | solution.py:22
  72.9 2.4 broadcast_multiply_fusion
  75.3 2.0 fusion.2
  77.3 3.5 %copy.10 = bf16[4,16,128,256]{3,2,1,0:T(8,128)(2,1)} copy(bf16[4,16,128,256]{3,1,2,0:T(8,128)(2,1)S(1)} %fusion.2) | data formatting | bytes 8388608 | tf_op jit(solution)/shard_map/while/body/eval_jaxpr/convert_element_type | solution.py:36
  80.9 9.0 %all-gather.6.cloned.1.call-done = bf16[256,2048]{1,0:T(8,128)(2,1)} async-done(((bf16[256,512]{1,0:T(8,128)(2,1)}), bf16[256,2048]{1,0:T(8,128)(2,1)}) %all-gather.6.cloned.1.call-update) | async-done | bytes 1048592 | tf_op jit(solution)/shard_map/all_gather | solution.py:12
  89.9 3.8 %convolution_negate_fusion = f32[4,256,256]{1,2,0:T(8,128)S(1)} fusion(bf16[4,2048,256]{2,1,0:T(8,128)(2,1)} %bitcast.23, bf16[256,2048]{1,0:T(8,128)(2,1)} %all-gather.6.cloned.1.call-done), kind=kOutput, calls=%fused_computation.7 | convolution fusion | flops 1074003968 | bytes 6291456 | tf_op jit(solution)/shard_map/while/body/eval_jaxpr/rw,gwc->grc/dot_general | solution.py:37
  93.7 4.4 %convolution_convert_fusion = bf16[4,12,128,256]{3,1,2,0:T(8,128)(2,1)S(1)} fusion(f32[4,2,128,256]{3,2,1,0:T(8,128)S(1)} %bitcast.24, pred[4,16,12]{2,1,0:T(8,128)(4,1)S(1)} %fusion.9, s32[]{:T(128)S(6)} %select_n.26), kind=kOutput, calls=%fused_computation.3 | convolution fusion | flops 39321600 | bytes 4196356 | tf_op jit(solution)/shard_map/while/body/eval_jaxpr/gjk,gjic->gkic/dot_general | solution.py:45
  98.1 2.9 %copy.12 = bf16[4,12,128,256]{3,2,1,0:T(8,128)(2,1)} copy(bf16[4,12,128,256]{3,1,2,0:T(8,128)(2,1)S(1)} %convolution_convert_fusion) | data formatting | bytes 6291456 | tf_op jit(solution)/shard_map/while/body/eval_jaxpr/convert_element_type | solution.py:54
  101.0 0.0 reduce-scatter.5.cloned.1.call-start
  101.1 0.5 copy-done.2
  101.6 0.1 compare_convert_fusion.1
  101.7 9.6 %all-gather.8.cloned.1.call-done = bf16[4,192,1024]{2,1,0:T(8,128)(2,1)} async-done(((bf16[4,192,256]{2,1,0:T(8,128)(2,1)}), bf16[4,192,1024]{2,1,0:T(8,128)(2,1)}) %all-gather.8.cloned.1.call-update) | async-done | bytes 1572880 | tf_op jit(solution)/shard_map/while/body/eval_jaxpr/all_gather | solution.py:56
  111.3 78.3 %reduce-scatter.3.cloned.1.call-done = bf16[4,192,256]{2,1,0:T(8,128)(2,1)} async-done(((bf16[4,1536,256]{2,1,0:T(8,128)(2,1)}), bf16[4,192,256]{2,1,0:T(8,128)(2,1)}) %reduce-scatter.3.cloned.1.call-update) | async-done | bytes 393232 | tf_op jit(solution)/shard_map/while/body/eval_jaxpr/reduce_scatter | solution.py:53
  189.6 3.8 %convolution_convert_fusion.1 = bf16[4,1024,256]{2,1,0:T(8,128)(2,1)} fusion(bf16[4,192,256]{2,1,0:T(8,128)(2,1)} %reduce-scatter.3.cloned.1.call-done, bf16[4,192,1024]{2,1,0:T(8,128)(2,1)} %all-gather.8.cloned.1.call-done, bf16[4,192]{1,0:T(4,128)(2,1)S(1)} %compare_convert_fusion.1), kind=kOutput, calls=%fused_computation.4 | convolution fusion | flops 404488192 | bytes 4064768 | tf_op jit(solution)/shard_map/while/body/eval_jaxpr/gka,gkc->gac/dot_general | solution.py:58
  193.5 68.0 %reduce-scatter.5.cloned.1.call-done = bf16[4,128,256]{2,1,0:T(8,128)(2,1)} async-done(((bf16[4,1024,256]{2,1,0:T(8,128)(2,1)}), bf16[4,128,256]{2,1,0:T(8,128)(2,1)}) %reduce-scatter.5.cloned.1.call-update) | async-done | bytes 262160 | tf_op jit(solution)/shard_map/while/body/eval_jaxpr/reduce_scatter | solution.py:61
  261.5 1.8 convert_subtract_fusion
  (11 shorter events, 0.1 us)
Async XLA Ops:
  7.2 65.8 %all-gather.4.cloned.1.call-start = ((), (), s32[]{:S(2)}) async-start(), calls=%async_computation.2 | async-start | bytes 3538944 | tf_op jit(solution)/shard_map/while/body/eval_jaxpr/all_gather | solution.py:22
  7.9 82.0 %all-gather.6.cloned.1.call-start = ((), (), s32[]{:S(2)}) async-start(), calls=%async_computation.3 | async-start | bytes 1310720 | tf_op jit(solution)/shard_map/all_gather | solution.py:12
  8.6 102.7 %all-gather.8.cloned.1.call-start = ((), (), s32[]{:S(2)}) async-start(), calls=%async_computation.5 | async-start | bytes 1966080 | tf_op jit(solution)/shard_map/while/body/eval_jaxpr/all_gather | solution.py:56
  9.4 180.2 %reduce-scatter.3.cloned.1.call-start = ((), (), s32[]{:S(2)}) async-start(), calls=%async_computation.4 | async-start | bytes 3538944 | tf_op jit(solution)/shard_map/while/body/eval_jaxpr/reduce_scatter | solution.py:53
  11.6 63.7 %copy-start.1 = (s32[4,12]{1,0:T(4,128)S(1)}, s32[4,12]{1,0:T(4,128)}, u32[]{:S(2)}) copy-start(s32[4,12]{1,0:T(4,128)} %param.7) | copy-start | bytes 580
  101.0 0.7 copy-start.2
  101.0 160.5 %copy-start = (f32[4,128,256]{2,1,0:T(8,128)S(1)}, f32[4,128,256]{2,1,0:T(8,128)}, u32[]{:S(2)}) copy-start(f32[4,128,256]{2,1,0:T(8,128)} %param.9) | copy-start | bytes 1572868
  101.0 160.5 %reduce-scatter.5.cloned.1.call-start = ((), (), s32[]{:S(2)}) async-start(), calls=%async_computation.6 | async-start | bytes 2359296 | tf_op jit(solution)/shard_map/while/body/eval_jaxpr/reduce_scatter | solution.py:61
Sparse Core Ops, SparseCore 0:
  10.2 62.7 all-gather.3
  74.5 15.3 all-gather.5
  91.5 19.8 all-gather.7
  115.3 74.2 reduce-scatter.2
  193.6 67.8 reduce-scatter.4
where the time goes:
time: 270 us
  waiting for transfers between devices  228 us (84%)
  matrix products  14 us (5%)
  between operations  13.8 us (5%)
  local copies, waits for them, and re-layouts  6.97 us (3%)
  other arithmetic  6.43 us (2%)
    reduce_scatter x1, waiting for transfers between devices, solve_group(): lax.psum_scatter(selected.astype(jnp.bfloat16), 'col', scatter_dimension=...  78.3 us
    reduce_scatter x1, waiting for transfers between devices, solve_group(): lax.psum_scatter(schur_terms.astype(jnp.bfloat16), 'col', scatter_dimensi...  68 us
    all_gather x1, waiting for transfers between devices, solve_group(): gathered = lax.all_gather(lower_group, 'col', axis=1, tiled=True)  61.3 us
    all_gather x1, waiting for transfers between devices, solve_group(): full_cols = lax.all_gather(lower_group, 'row', axis=2, tiled=True)  9.62 us
    all_gather x1, waiting for transfers between devices, body(): root_panel = lax.all_gather(root_inverse, 'row', axis=1, tiled=True)  9.03 us
  transfers between devices with their start and end apart: 5, of which 5 were waited for; matrix products, arithmetic and copies ran while one was open for 8% of the time, Pallas kernels for 0%

commit v1 on v0

--- a/solution.py
+++ b/solution.py
@@ -19,7 +19,14 @@
     def solve_group(lower_group, block_lists, block_counts, inverse_group):
         group_size = lower_group.shape[0]
         cols_here = lower_group.shape[2]
-        gathered = lax.all_gather(lower_group, "col", axis=1, tiled=True)
+        ring = [lower_group]
+        for hop in range(7):
+            ring.append(lax.ppermute(ring[-1], "col", [(dev, (dev + 1) % 8) for dev in range(8)]))
+        gathered = jnp.roll(
+            jnp.concatenate(ring[::-1], axis=1),
+            (lax.axis_index("col") + 1) * ring[0].shape[1],
+            axis=1,
+        )
         packed_total = gathered.shape[1]
         full_mask = jnp.arange(packed_total)[None, :] // BLOCK < block_counts[:, None]
         gathered = gathered * full_mask[:, :, None].astype(jnp.bfloat16)

time: 270 us -> 261 us (0.967)
  waiting for transfers between devices: 228 us -> 218 us
  starting transfers between devices: 0.19 us -> 3.2 us
    ppermute x0 -> x7, waiting for transfers between devices: none -> 78.1 us  [solve_group(): lax.ppermute(ring[-1], 'col', [(dev, (dev + 1) % 8) for dev in range(8)])]
    all_gather x1 -> x0, waiting for transfers between devices: 61.3 us -> none  [solve_group(): gathered = lax.all_gather(lower_group, 'col', axis=1, tiled=True)]
    all_gather x1, waiting for transfers between devices: 9.62 us -> 0.01 us  [solve_group(): full_cols = lax.all_gather(lower_group, 'row', axis=2, tiled=True)]
    all_gather x1, waiting for transfers between devices: 9.03 us -> 0.01 us  [body(): root_panel = lax.all_gather(root_inverse, 'row', axis=1, tiled=True)]
    reduce_scatter x1, waiting for transfers between devices: 78.3 us -> 71.3 us  [solve_group(): lax.psum_scatter(selected.astype(jnp.bfloat16), 'col', scatter_dimension=...]
    ppermute x0 -> x7, starting transfers between devices: none -> 3.04 us  [solve_group(): lax.ppermute(ring[-1], 'col', [(dev, (dev + 1) % 8) for dev in range(8)])]
  transfers between devices with their start and end apart: 5 -> 11, of which waited for: 5 -> 9; matrix products, arithmetic and copies ran while one was open for 8% -> 8% of each run, Pallas kernels for 0% -> 0%
where the time goes in v1:
time: 261 us
  waiting for transfers between devices  218 us (84%)
  matrix products  14 us (5%)
  between operations  14 us (5%)
  local copies, waits for them, and re-layouts  6.91 us (3%)
  other arithmetic  5.38 us (2%)
  starting transfers between devices  3.2 us (1%)
    ppermute x7, waiting for transfers between devices, solve_group(): lax.ppermute(ring[-1], 'col', [(dev, (dev + 1) % 8) for dev in range(8)])  78.1 us
    reduce_scatter x1, waiting for transfers between devices, solve_group(): lax.psum_scatter(selected.astype(jnp.bfloat16), 'col', scatter_dimension=...  71.3 us
    reduce_scatter x1, waiting for transfers between devices, solve_group(): lax.psum_scatter(schur_terms.astype(jnp.bfloat16), 'col', scatter_dimensi...  68.1 us
  transfers between devices with their start and end apart: 11, of which 9 were waited for; matrix products, arithmetic and copies ran while one was open for 8% of the time, Pallas kernels for 0%

profile of v1, /device:TPU:0, one launch (start us, length us, event | category | flops | bytes accessed | tf_op | source)
XLA Modules:
  0.0 261.1 jit_solution(9844098853699714822)
XLA Ops:
  7.2 3.0 %collective-permute-start = (bf16[4,192,256]{2,1,0:T(8,128)(2,1)}, bf16[4,192,256]{2,1,0:T(8,128)(2,1)S(1)}, u32[]{:S(2)}, u32[]{:S(2)}) collective-permute-start(bf16[4,192,256]{2,1,0:T(8,128)(2,1)} %param.6), channel_id=1, source_target_pairs={{0,1},{1,2},{2,3},{3,4},{4,5},{5,6},{6,7},{7,0},{8,9},{9,10},{10,1... | collective-permute-start | bytes 1179656 | tf_op jit(solution)/shard_map/while/body/eval_jaxpr/ppermute | solution.py:24
  10.3 0.0 all-gather.5.cloned.1.call-start
  10.3 12.3 %collective-permute-done = bf16[4,192,256]{2,1,0:T(8,128)(2,1)S(1)} collective-permute-done((bf16[4,192,256]{2,1,0:T(8,128)(2,1)}, bf16[4,192,256]{2,1,0:T(8,128)(2,1)S(1)}, u32[]{:S(2)}, u32[]{:S(2)}) %collective-permute-start) | collective-permute-done | bytes 393248 | tf_op jit(solution)/shard_map/while/body/eval_jaxpr/ppermute | solution.py:24
  22.6 13.0 %collective-permute-done.1 = bf16[4,192,256]{2,1,0:T(8,128)(2,1)S(1)} collective-permute-done((bf16[4,192,256]{2,1,0:T(8,128)(2,1)S(1)}, bf16[4,192,256]{2,1,0:T(8,128)(2,1)S(1)}, u32[]{:S(2)}, u32[]{:S(2)}) %collective-permute-start.1) | collective-permute-done | bytes 393248 | tf_op jit(solution)/shard_map/while/body/eval_jaxpr/ppermute | solution.py:24
  35.6 12.1 %collective-permute-done.2 = bf16[4,192,256]{2,1,0:T(8,128)(2,1)S(1)} collective-permute-done((bf16[4,192,256]{2,1,0:T(8,128)(2,1)S(1)}, bf16[4,192,256]{2,1,0:T(8,128)(2,1)S(1)}, u32[]{:S(2)}, u32[]{:S(2)}) %collective-permute-start.2) | collective-permute-done | bytes 393248 | tf_op jit(solution)/shard_map/while/body/eval_jaxpr/ppermute | solution.py:24
  47.7 11.3 %collective-permute-done.3 = bf16[4,192,256]{2,1,0:T(8,128)(2,1)S(1)} collective-permute-done((bf16[4,192,256]{2,1,0:T(8,128)(2,1)S(1)}, bf16[4,192,256]{2,1,0:T(8,128)(2,1)S(1)}, u32[]{:S(2)}, u32[]{:S(2)}) %collective-permute-start.3) | collective-permute-done | bytes 393248 | tf_op jit(solution)/shard_map/while/body/eval_jaxpr/ppermute | solution.py:24
  59.1 10.4 %collective-permute-done.4 = bf16[4,192,256]{2,1,0:T(8,128)(2,1)S(1)} collective-permute-done((bf16[4,192,256]{2,1,0:T(8,128)(2,1)S(1)}, bf16[4,192,256]{2,1,0:T(8,128)(2,1)S(1)}, u32[]{:S(2)}, u32[]{:S(2)}) %collective-permute-start.4) | collective-permute-done | bytes 393248 | tf_op jit(solution)/shard_map/while/body/eval_jaxpr/ppermute | solution.py:24
  69.4 0.7 iota_compare_fusion.1
  70.2 0.7 fusion.9
  70.9 9.4 %collective-permute-done.5 = bf16[4,192,256]{2,1,0:T(8,128)(2,1)S(1)} collective-permute-done((bf16[4,192,256]{2,1,0:T(8,128)(2,1)S(1)}, bf16[4,192,256]{2,1,0:T(8,128)(2,1)S(1)}, u32[]{:S(2)}, u32[]{:S(2)}) %collective-permute-start.5) | collective-permute-done | bytes 393248 | tf_op jit(solution)/shard_map/while/body/eval_jaxpr/ppermute | solution.py:24
  80.2 0.7 compare_convert_fusion
  81.0 9.7 %collective-permute-done.6 = bf16[4,192,256]{2,1,0:T(8,128)(2,1)S(1)} collective-permute-done((bf16[4,192,256]{2,1,0:T(8,128)(2,1)S(1)}, bf16[4,192,256]{2,1,0:T(8,128)(2,1)S(1)}, u32[]{:S(2)}, u32[]{:S(2)}) %collective-permute-start.6) | collective-permute-done | bytes 393248 | tf_op jit(solution)/shard_map/while/body/eval_jaxpr/ppermute | solution.py:24
  91.3 1.3 dynamic-slice_multiply_fusion
  92.6 2.0 fusion.2
  94.6 3.5 %copy.10 = bf16[4,16,128,256]{3,2,1,0:T(8,128)(2,1)} copy(bf16[4,16,128,256]{3,1,2,0:T(8,128)(2,1)S(1)} %fusion.2) | data formatting | bytes 8388608 | tf_op jit(solution)/shard_map/while/body/eval_jaxpr/convert_element_type | solution.py:43
  98.2 3.8 %convolution_negate_fusion = f32[4,256,256]{1,2,0:T(8,128)S(1)} fusion(bf16[4,2048,256]{2,1,0:T(8,128)(2,1)} %bitcast.23, bf16[256,2048]{1,0:T(8,128)(2,1)} %all-gather.3.cloned.1.call-done), kind=kOutput, calls=%fused_computation.7 | convolution fusion | flops 1074003968 | bytes 6291456 | tf_op jit(solution)/shard_map/while/body/eval_jaxpr/rw,gwc->grc/dot_general | solution.py:44
  102.0 4.4 %convolution_convert_fusion = bf16[4,12,128,256]{3,1,2,0:T(8,128)(2,1)S(1)} fusion(f32[4,2,128,256]{3,2,1,0:T(8,128)S(1)} %bitcast.24, pred[4,16,12]{2,1,0:T(8,128)(4,1)S(1)} %fusion.9, s32[]{:T(128)S(6)} %select_n.42), kind=kOutput, calls=%fused_computation.4 | convolution fusion | flops 39321600 | bytes 4196356 | tf_op jit(solution)/shard_map/while/body/eval_jaxpr/gjk,gjic->gkic/dot_general | solution.py:52
  106.4 2.9 %copy.12 = bf16[4,12,128,256]{3,2,1,0:T(8,128)(2,1)} copy(bf16[4,12,128,256]{3,1,2,0:T(8,128)(2,1)S(1)} %convolution_convert_fusion) | data formatting | bytes 6291456 | tf_op jit(solution)/shard_map/while/body/eval_jaxpr/convert_element_type | solution.py:61
  109.3 0.0 reduce-scatter.5.cloned.1.call-start
  109.4 0.1 compare_convert_fusion.1
  109.5 71.3 %reduce-scatter.3.cloned.1.call-done = bf16[4,192,256]{2,1,0:T(8,128)(2,1)} async-done(((bf16[4,1536,256]{2,1,0:T(8,128)(2,1)}), bf16[4,192,256]{2,1,0:T(8,128)(2,1)}) %reduce-scatter.3.cloned.1.call-update) | async-done | bytes 393232 | tf_op jit(solution)/shard_map/while/body/eval_jaxpr/reduce_scatter | solution.py:60
  180.7 3.9 %convolution_convert_fusion.1 = bf16[4,1024,256]{2,1,0:T(8,128)(2,1)} fusion(bf16[4,192,256]{2,1,0:T(8,128)(2,1)} %reduce-scatter.3.cloned.1.call-done, bf16[4,192,1024]{2,1,0:T(8,128)(2,1)} %all-gather.5.cloned.1.call-done, bf16[4,192]{1,0:T(4,128)(2,1)S(1)} %compare_convert_fusion.1), kind=kOutput, calls=%fused_computation.5 | convolution fusion | flops 404488192 | bytes 4064768 | tf_op jit(solution)/shard_map/while/body/eval_jaxpr/gka,gkc->gac/dot_general | solution.py:65
  184.6 68.1 %reduce-scatter.5.cloned.1.call-done = bf16[4,128,256]{2,1,0:T(8,128)(2,1)} async-done(((bf16[4,1024,256]{2,1,0:T(8,128)(2,1)}), bf16[4,128,256]{2,1,0:T(8,128)(2,1)}) %reduce-scatter.5.cloned.1.call-update) | async-done | bytes 262160 | tf_op jit(solution)/shard_map/while/body/eval_jaxpr/reduce_scatter | solution.py:68
  252.7 1.8 convert_subtract_fusion
  (40 shorter events, 0.6 us)
Async XLA Ops:
  7.2 83.8 %copy-start = (bf16[4,192,256]{2,1,0:T(8,128)(2,1)S(1)}, bf16[4,192,256]{2,1,0:T(8,128)(2,1)}, u32[]{:S(2)}) copy-start(bf16[4,192,256]{2,1,0:T(8,128)(2,1)} %param.6) | copy-start | bytes 1179652
  7.2 91.0 %all-gather.3.cloned.1.call-start = ((), (), s32[]{:S(2)}) async-start(), calls=%async_computation.2 | async-start | bytes 1310720 | tf_op jit(solution)/shard_map/all_gather | solution.py:12
  7.2 15.4 %collective-permute-start = (bf16[4,192,256]{2,1,0:T(8,128)(2,1)}, bf16[4,192,256]{2,1,0:T(8,128)(2,1)S(1)}, u32[]{:S(2)}, u32[]{:S(2)}) collective-permute-start(bf16[4,192,256]{2,1,0:T(8,128)(2,1)} %param.6), channel_id=1, source_target_pairs={{0,1},{1,2},{2,3},{3,4},{4,5},{5,6},{6,7},{7,0},{8,9},{9,10},{10,1... | collective-permute-start | bytes 1179656 | tf_op jit(solution)/shard_map/while/body/eval_jaxpr/ppermute | solution.py:24
  10.3 99.2 %all-gather.5.cloned.1.call-start = ((), (), s32[]{:S(2)}) async-start(), calls=%async_computation.4 | async-start | bytes 1966080 | tf_op jit(solution)/shard_map/while/body/eval_jaxpr/all_gather | solution.py:63
  22.6 13.0 %collective-permute-start.1 = (bf16[4,192,256]{2,1,0:T(8,128)(2,1)S(1)}, bf16[4,192,256]{2,1,0:T(8,128)(2,1)S(1)}, u32[]{:S(2)}, u32[]{:S(2)}) collective-permute-start(bf16[4,192,256]{2,1,0:T(8,128)(2,1)S(1)} %collective-permute-done), channel_id=1, source_target_pairs={{0,1},{1,2},{2,3},{3,4},{4,5},{5,6},{6,7},{7,0},{8,9},{9,10},{10,1... | collective-permute-start | bytes 1179656 | tf_op jit(solution)/shard_map/while/body/eval_jaxpr/ppermute | solution.py:24
  35.6 12.1 %collective-permute-start.2 = (bf16[4,192,256]{2,1,0:T(8,128)(2,1)S(1)}, bf16[4,192,256]{2,1,0:T(8,128)(2,1)S(1)}, u32[]{:S(2)}, u32[]{:S(2)}) collective-permute-start(bf16[4,192,256]{2,1,0:T(8,128)(2,1)S(1)} %collective-permute-done.1), channel_id=1, source_target_pairs={{0,1},{1,2},{2,3},{3,4},{4,5},{5,6},{6,7},{7,0},{8,9},{9,10},{10,1... | collective-permute-start | bytes 1179656 | tf_op jit(solution)/shard_map/while/body/eval_jaxpr/ppermute | solution.py:24
  47.7 11.3 %collective-permute-start.3 = (bf16[4,192,256]{2,1,0:T(8,128)(2,1)S(1)}, bf16[4,192,256]{2,1,0:T(8,128)(2,1)S(1)}, u32[]{:S(2)}, u32[]{:S(2)}) collective-permute-start(bf16[4,192,256]{2,1,0:T(8,128)(2,1)S(1)} %collective-permute-done.2), channel_id=1, source_target_pairs={{0,1},{1,2},{2,3},{3,4},{4,5},{5,6},{6,7},{7,0},{8,9},{9,10},{10,1... | collective-permute-start | bytes 1179656 | tf_op jit(solution)/shard_map/while/body/eval_jaxpr/ppermute | solution.py:24
  59.0 10.5 %collective-permute-start.4 = (bf16[4,192,256]{2,1,0:T(8,128)(2,1)S(1)}, bf16[4,192,256]{2,1,0:T(8,128)(2,1)S(1)}, u32[]{:S(2)}, u32[]{:S(2)}) collective-permute-start(bf16[4,192,256]{2,1,0:T(8,128)(2,1)S(1)} %collective-permute-done.3), channel_id=1, source_target_pairs={{0,1},{1,2},{2,3},{3,4},{4,5},{5,6},{6,7},{7,0},{8,9},{9,10},{10,1... | collective-permute-start | bytes 1179656 | tf_op jit(solution)/shard_map/while/body/eval_jaxpr/ppermute | solution.py:24
  59.0 121.8 %reduce-scatter.3.cloned.1.call-start = ((), (), s32[]{:S(2)}) async-start(), calls=%async_computation.3 | async-start | bytes 3538944 | tf_op jit(solution)/shard_map/while/body/eval_jaxpr/reduce_scatter | solution.py:60
  69.4 10.8 %collective-permute-start.5 = (bf16[4,192,256]{2,1,0:T(8,128)(2,1)S(1)}, bf16[4,192,256]{2,1,0:T(8,128)(2,1)S(1)}, u32[]{:S(2)}, u32[]{:S(2)}) collective-permute-start(bf16[4,192,256]{2,1,0:T(8,128)(2,1)S(1)} %collective-permute-done.4), channel_id=1, source_target_pairs={{0,1},{1,2},{2,3},{3,4},{4,5},{5,6},{6,7},{7,0},{8,9},{9,10},{10,1... | collective-permute-start | bytes 1179656 | tf_op jit(solution)/shard_map/while/body/eval_jaxpr/ppermute | solution.py:24
  80.2 10.5 %collective-permute-start.6 = (bf16[4,192,256]{2,1,0:T(8,128)(2,1)S(1)}, bf16[4,192,256]{2,1,0:T(8,128)(2,1)S(1)}, u32[]{:S(2)}, u32[]{:S(2)}) collective-permute-start(bf16[4,192,256]{2,1,0:T(8,128)(2,1)S(1)} %collective-permute-done.5), channel_id=1, source_target_pairs={{0,1},{1,2},{2,3},{3,4},{4,5},{5,6},{6,7},{7,0},{8,9},{9,10},{10,1... | collective-permute-start | bytes 1179656 | tf_op jit(solution)/shard_map/while/body/eval_jaxpr/ppermute | solution.py:24
  91.0 1.6 copy-start.2
  106.4 3.0 %copy-start.3 = (s32[4]{0:T(128)S(1)}, s32[4]{0:T(128)}, u32[]{:S(2)}) copy-start(s32[4]{0:T(128)} %param.8) | copy-start | bytes 52
  109.3 143.4 %copy-start.1 = (f32[4,128,256]{2,1,0:T(8,128)S(1)}, f32[4,128,256]{2,1,0:T(8,128)}, u32[]{:S(2)}) copy-start(f32[4,128,256]{2,1,0:T(8,128)} %param.9) | copy-start | bytes 1572868
  109.3 143.4 %reduce-scatter.5.cloned.1.call-start = ((), (), s32[]{:S(2)}) async-start(), calls=%async_computation.5 | async-start | bytes 2359296 | tf_op jit(solution)/shard_map/while/body/eval_jaxpr/reduce_scatter | solution.py:68
Sparse Core Ops, SparseCore 0:
  10.4 18.5 all-gather.2
  59.1 20.6 all-gather.4
  109.4 71.2 reduce-scatter.2
  184.8 67.9 reduce-scatter.4
